TPU v7x, 32 devices: a whole 2x2x4 slice. The times are simulated.
32 devices in a mesh: member: 2 (over x), gx: 16 (over z, y, core).
Axes of the slice: x: 2, y: 2, z: 4, core: 2. Of those that a mesh axis runs over, the one named last changes fastest.
Arguments:
- spectrum: float32 [36, 32, 256, 128], P(None, None, ('member', 'gx')), parts along dimension 2, may hold values from 0 to 1
- wind: float32 [2, 256, 128], P(None, ('member', 'gx')), parts along dimension 1, may hold values from -32 to 32
- land_sea: int32 [128, 128], P('gx'), may hold values 0 or 1
- band_rows: int32 [128], replicated, may hold values from 0 to 127, each once
Outputs:
- spectrum_next: float32 [36, 32, 256, 128], P(None, None, ('member', 'gx')), parts along dimension 2
- ocean_fields: float32 [4, 128, 256], P(None, 'gx', 'member'), parts along dimension 2
There are 2 independent parts, one for each index of `member`. A program takes and returns all parts, laid end to end along the dimension named above; an argument that names none is the same for every part. Nothing has to cross between parts.
Inputs may be any that keep to these rules, and one draw needn't show every extreme that they name: band_rows names each of the 128 latitude rows exactly once.
All inputs are finite; a program needn't handle non-finite values. No bound on the sum of `land_sea` on one device may be relied on, other than what follows from the above.
Results may differ from a plain program's by a relative error of at most 0.00015.
Values sent between devices are 32-bit elements; how exact they have to be, the bound alone decides.
A program may use at most 128 MiB of HBM per device.

v0:
```python
import math

import jax
import jax.numpy as jnp
from jax import lax
from jax.sharding import PartitionSpec as P

STEPS = 3


def passed_along(value, axis, steps):
    count = lax.axis_size(axis)
    pairs = [(source, (source + steps) % count) for source in range(count)]
    return lax.ppermute(value, axis, pairs)


def wave_tables(directions, frequencies):
    angles = (jnp.arange(directions, dtype=jnp.float32) + 0.5) * (2.0 * math.pi / directions)
    levels = jnp.arange(frequencies, dtype=jnp.float32)
    shrink = jnp.power(jnp.float32(1.1), -levels)
    frequency = 0.0418 / shrink
    inverse_speed = 2.0 * math.pi * frequency / 9.81
    weight = (levels + 1.0) / frequencies
    cosine_dir = jnp.cos(angles)[:, None]
    sine_dir = jnp.sin(angles)[:, None]
    courant_x = 0.45 * shrink[None, :] * cosine_dir
    courant_y = 0.45 * shrink[None, :] * sine_dir
    factor = 3.0 / math.sqrt(directions * frequencies)
    project = jnp.stack(
        [factor * weight[None, :] * cosine_dir, factor * weight[None, :] * sine_dir]
    )
    return (courant_x, courant_y, cosine_dir, sine_dir, inverse_speed, weight * weight, project)


def upwind(center, west_cell, east_cell, courant_x, courant_y):
    along_x = courant_x[:, :, None, None]
    along_y = courant_y[:, :, None, None]
    border = jnp.zeros_like(center[..., :1])
    south_cell = jnp.concatenate([border, center[..., :-1]], axis=3)
    north_cell = jnp.concatenate([center[..., 1:], border], axis=3)
    return (
        center
        - jnp.maximum(along_x, 0.0) * (center - west_cell)
        + jnp.maximum(-along_x, 0.0) * (east_cell - center)
        - jnp.maximum(along_y, 0.0) * (center - south_cell)
        + jnp.maximum(-along_y, 0.0) * (north_cell - center)
    )


def sources(advected, wind_east, wind_north, sea_mask, tables):
    cosine_dir, sine_dir, inverse_speed, weight_two = (tables[2], tables[3], tables[4], tables[5])
    advected = advected * sea_mask
    energy = jnp.mean(advected, axis=(0, 1))
    wind_ratio = (
        wind_east * cosine_dir[:, :, None, None] + wind_north * sine_dir[:, :, None, None]
    ) * inverse_speed[None, :, None, None]
    growth = 0.05 * jnp.clip(wind_ratio - 1.0, 0.0, 4.0)
    damping = 0.3 * weight_two[None, :, None, None] * (energy / (0.5 + energy))
    return (advected * (1.0 + growth) / (1.0 + damping), growth * advected)


def coupling_fields(input_flux, current, project):
    stress = jnp.einsum("cij,ijxy->cxy", project, input_flux, precision=lax.Precision.HIGHEST)
    stokes = jnp.einsum("cij,ijxy->cxy", project, current, precision=lax.Precision.HIGHEST)
    return jnp.concatenate([stress, stokes], axis=0)


def per_device(spectrum, wind, land_sea, band_rows):
    tables = wave_tables(spectrum.shape[0], spectrum.shape[1])
    sea_mask = land_sea.astype(jnp.float32)
    current = spectrum
    quarter = spectrum.shape[0] // 4
    east_x = jnp.concatenate([tables[0][:quarter], tables[0][3 * quarter :]], axis=0)
    east_y = jnp.concatenate([tables[1][:quarter], tables[1][3 * quarter :]], axis=0)
    west_x = tables[0][quarter : 3 * quarter]
    west_y = tables[1][quarter : 3 * quarter]
    for step_index in range(STEPS):
        eastward = jnp.concatenate([current[:quarter], current[3 * quarter :]], axis=0)
        westward = current[quarter : 3 * quarter]
        from_west = passed_along(eastward[:, :, -1:], "gx", 1)
        from_east = passed_along(westward[:, :, :1], "gx", -1)
        west_cells = jnp.concatenate([from_west, eastward[:, :, :-1]], axis=2)
        east_cells = jnp.concatenate([westward[:, :, 1:], from_east], axis=2)
        moved_east = upwind(eastward, west_cells, eastward, east_x, east_y)
        moved_west = upwind(westward, westward, east_cells, west_x, west_y)
        advected = jnp.concatenate([moved_east[:quarter], moved_west, moved_east[quarter:]], axis=0)
        current, input_flux = sources(advected, wind[0], wind[1], sea_mask, tables)
    fields = coupling_fields(input_flux, current, tables[6])
    local_rows = jnp.transpose(fields[:, :, band_rows], (0, 2, 1))
    gathered = lax.all_gather(local_rows, "gx", axis=2, tiled=True)
    band_count = local_rows.shape[1] // lax.axis_size("gx")
    ocean_fields = lax.dynamic_slice_in_dim(
        gathered, lax.axis_index("gx") * band_count, band_count, 1
    )
    return (current, ocean_fields)


def solution(mesh):
    placed = (
        P(None, None, ("member", "gx"), None),
        P(None, ("member", "gx"), None),
        P("gx", None),
        P(),
    )
    return jax.shard_map(
        per_device,
        mesh=mesh,
        in_specs=placed,
        out_specs=(P(None, None, ("member", "gx"), None), P(None, "gx", "member")),
        check_vma=False,
    )
```

profile of v0, /device:TPU:0, one launch (start us, length us, event | category | flops | bytes accessed | tf_op | source)
XLA Modules:
  0.0 96.4 jit_solution(8376153678232764763)
XLA Ops:
  0.6 1.8 %fusion.60 = (f32[9,32,8,128]{3,2,1,0:T(8,128)S(1)}, f32[9,32,8,128]{3,2,1,0:T(8,128)S(1)}) fusion(f32[36,32,8,128]{3,2,1,0:T(8,128)} %param.4), kind=kLoop, calls=%fused_computation.121 | loop fusion | bytes 4718592 | tf_op jit(solution)/shard_map/slice | solution.py:78
  2.4 0.2 copy_dynamic-update-slice_fusion.1
  2.6 0.2 copy_dynamic-update-slice_fusion
  2.9 0.7 slice.228
  3.6 0.5 collective-permute-start
  4.1 0.8 copy-done
  4.9 0.2 slice.191
  5.1 5.5 %collective-permute-start.1 = (f32[18,32,1,128]{3,1,2,0:T(8,128)S(1)}, f32[18,32,1,128]{3,1,2,0:T(8,128)S(1)}, u32[]{:S(2)}, u32[]{:S(2)}) collective-permute-start(f32[18,32,1,128]{3,1,2,0:T(8,128)S(1)} %bitcast.18), channel_id=1, source_target_pairs={{0,15},{1,0},{2,1},{3,2},{4,3},{5,4},{6,5},{7,6},{8,7},{9,8},{10,9... | collective-permute-start | bytes 884744 | tf_op jit(solution)/shard_map/ppermute | solution.py:14
  10.6 3.1 %fusion.64 = (f32[18,32,8,127]{3,1,2,0:T(8,128)}, f32[18,32,8,127]{3,1,2,0:T(8,128)}) fusion(f32[18,32,8,128]{3,1,2,0:T(8,128)S(1)} %copy_dynamic-update-slice_fusion), kind=kLoop, calls=%fused_computation.125 | loop fusion | bytes 9363456 | tf_op jit(solution)/shard_map/slice | solution.py:39
  13.7 1.6 %slice.229 = f32[18,32,7,128]{3,1,2,0:T(8,128)} slice(f32[18,32,8,128]{3,1,2,0:T(8,128)S(1)} %copy_dynamic-update-slice_fusion), slice={[0:18], [0:32], [0:7], [0:128]} | slice | bytes 4128768 | tf_op jit(solution)/shard_map/slice | solution.py:82
  15.4 0.1 broadcast_multiply_fusion.1
  15.5 0.8 fusion.59
  16.3 0.2 slice.190
  16.6 1.8 %copy.58 = f32[18,32,8,127]{3,1,2,0:T(8,128)} copy(f32[18,32,8,127]{3,2,1,0:T(8,128)S(1)} %get-tuple-element.20) | data formatting | bytes 4681728
  18.5 1.9 %copy.59 = f32[18,32,8,127]{3,1,2,0:T(8,128)} copy(f32[18,32,8,127]{3,2,1,0:T(8,128)S(1)} %get-tuple-element.21) | data formatting | bytes 4681728
  20.3 1.7 %copy.56 = f32[18,32,7,128]{3,1,2,0:T(8,128)} copy(f32[18,32,7,128]{3,2,1,0:T(8,128)S(1)} %slice.190) | data formatting | bytes 4128768
  22.0 0.1 broadcast_multiply_fusion.3
  22.1 0.1 copy.41
  22.2 0.1 multiply_add_fusion
  22.4 4.0 %fusion.16 = f32[18,32,8,128]{3,1,2,0:T(8,128)S(1)} fusion(f32[18,32,8,128]{3,1,2,0:T(8,128)S(1)} %copy_dynamic-update-slice_fusion, f32[18,32,7,128]{3,1,2,0:T(8,128)} %slice.229, f32[18,32,1,128]{3,1,2,0:T(8,128)S(1)} %collective-permute-done, f32[18,32,8,127]{3,1,2,0:T(8,128)} %get-tuple-element.35, f32[18,32,8,127]{3,1,2,0:T(8,128)} %get-tuple-element.34, ...), kind=kLoop, calls=%fused_computation.43 | loop fusion | flops 7667712 | bytes 11768832 | tf_op jit(solution)/shard_map/add | solution.py:42
  26.4 0.3 fusion.63
  26.7 1.4 %slice-done = f32[18,32,8,128]{3,2,1,0:T(8,128)S(1)} async-done(((f32[36,32,8,128]{3,2,1,0:T(8,128)}), f32[18,32,8,128]{3,2,1,0:T(8,128)S(1)}, s32[]{:S(2)}) %slice-start) | async-done | bytes 2359320 | tf_op jit(solution)/shard_map/slice | solution.py:79
  28.1 0.7 copy-done.1
  28.8 1.7 %fusion.20 = f32[18,32,8,128]{3,1,2,0:T(8,128)S(1)} fusion(f32[18,32,1,128]{3,1,2,0:T(8,128)S(1)} %collective-permute-done.1, f32[18,32,7,128]{3,1,2,0:T(8,128)S(1)} %copy-done.3, f32[18,32,8,127]{3,1,2,0:T(8,128)S(1)} %copy-done.2, f32[18,32,8,127]{3,1,2,0:T(8,128)S(1)} %copy-done.1, f32[18,32,8,128]{3,2,1,0:T(8,128)S(1)} %slice-done, ...), kind=kLoop, calls=%fused_computation.48 | loop fusion | flops 7667712 | bytes 11768832 | tf_op jit(solution)/shard_map/add | solution.py:42
  30.6 0.6 fusion.7
  31.2 0.1 multiply_add_fusion.3
  31.2 1.4 %multiply_divide_fusion.2 = f32[36,32,8,128]{3,1,2,0:T(8,128)S(1)} fusion(f32[9,32,8,128]{3,1,2,0:T(8,128)S(1)} %get-tuple-element.33, f32[18,32,8,128]{3,1,2,0:T(8,128)S(1)} %fusion.20, f32[9,32,8,128]{3,1,2,0:T(8,128)S(1)} %get-tuple-element.32, f32[32,8,128]{2,0,1:T(8,128)S(1)} %multiply_add_fusion.3, f32[32]{0:T(128)S(1)} %power_multiply_fusion, ...), kind=kLoop, calls=%fused_computation.10 | loop fusion | flops 11796480 | bytes 9719936 | tf_op jit(solution)/shard_map/div | solution.py:59
  32.6 0.9 fusion.57
  33.5 0.3 fusion.58
  33.8 0.1 collective-permute-start.2
  33.9 0.2 fusion.40
  34.2 0.2 slice.250
  34.4 4.7 %collective-permute-start.3 = (f32[18,32,1,128]{3,1,2,0:T(8,128)S(1)}, f32[18,32,1,128]{3,1,2,0:T(8,128)S(1)}, u32[]{:S(2)}, u32[]{:S(2)}) collective-permute-start(f32[18,32,1,128]{3,1,2,0:T(8,128)S(1)} %slice.251), channel_id=1, source_target_pairs={{0,15},{1,0},{2,1},{3,2},{4,3},{5,4},{6,5},{7,6},{8,7},{9,8},{10,9... | collective-permute-start | bytes 884744 | tf_op jit(solution)/shard_map/ppermute | solution.py:14
  39.1 0.9 fusion.10
  39.9 2.8 %collective-permute-done.2 = f32[18,32,1,128]{3,1,2,0:T(8,128)S(1)} collective-permute-done((f32[18,32,1,128]{3,1,2,0:T(8,128)S(1)}, f32[18,32,1,128]{3,1,2,0:T(8,128)S(1)}, u32[]{:S(2)}, u32[]{:S(2)}) %collective-permute-start.2) | collective-permute-done | bytes 294944 | tf_op jit(solution)/shard_map/ppermute | solution.py:14
  42.7 1.9 %fusion.25 = f32[18,32,8,128]{3,1,2,0:T(8,128)S(1)} fusion(f32[18,32,7,128]{3,1,2,0:T(8,128)S(1)} %fusion.40, f32[18,32,1,128]{3,1,2,0:T(8,128)S(1)} %collective-permute-done.2, f32[18,32,8,127]{3,1,2,0:T(8,128)S(1)} %get-tuple-element.31, f32[18,32,8,127]{3,1,2,0:T(8,128)S(1)} %get-tuple-element.30, f32[9,32,8,128]{3,1,2,0:T(8,128)S(1)} %get-tuple-element.18, ...), kind=kLoop, calls=%fused_computation.54 | loop fusion | flops 8257536 | bytes 11768832 | tf_op jit(solution)/shard_map/add | solution.py:42
  44.7 0.2 fusion.62
  44.9 1.8 %fusion.29 = f32[18,32,8,128]{3,1,2,0:T(8,128)S(1)} fusion(f32[18,32,1,128]{3,1,2,0:T(8,128)S(1)} %collective-permute-done.3, f32[18,32,7,128]{3,1,2,0:T(8,128)S(1)} %slice.250, f32[18,32,8,127]{3,1,2,0:T(8,128)S(1)} %get-tuple-element.17, f32[18,32,8,127]{3,1,2,0:T(8,128)S(1)} %get-tuple-element.16, f32[36,32,8,128]{3,1,2,0:T(8,128)S(1)} %multiply_divide_fusion.2, ...), kind=kLoop, calls=%fused_computation.59 | loop fusion | flops 7667712 | bytes 11768832 | tf_op jit(solution)/shard_map/add | solution.py:42
  46.7 0.6 fusion.6
  47.3 0.1 multiply_add_fusion.2
  47.4 1.4 %multiply_divide_fusion.1 = f32[36,32,8,128]{3,1,2,0:T(8,128)S(1)} fusion(f32[9,32,8,128]{3,1,2,0:T(8,128)S(1)} %get-tuple-element.29, f32[18,32,8,128]{3,1,2,0:T(8,128)S(1)} %fusion.29, f32[9,32,8,128]{3,1,2,0:T(8,128)S(1)} %get-tuple-element.28, f32[32,8,128]{2,0,1:T(8,128)S(1)} %multiply_add_fusion.2, f32[32]{0:T(128)S(1)} %power_multiply_fusion, ...), kind=kLoop, calls=%fused_computation.9 | loop fusion | flops 11796480 | bytes 9719936 | tf_op jit(solution)/shard_map/div | solution.py:59
  48.8 0.9 fusion.55
  49.6 0.3 fusion.56
  50.0 0.1 collective-permute-start.4
  50.0 0.2 fusion.39
  50.3 0.2 slice.267
  50.5 4.5 %collective-permute-start.5 = (f32[18,32,1,128]{3,1,2,0:T(8,128)S(1)}, f32[18,32,1,128]{3,1,2,0:T(8,128)S(1)}, u32[]{:S(2)}, u32[]{:S(2)}) collective-permute-start(f32[18,32,1,128]{3,1,2,0:T(8,128)S(1)} %slice.268), channel_id=1, source_target_pairs={{0,15},{1,0},{2,1},{3,2},{4,3},{5,4},{6,5},{7,6},{8,7},{9,8},{10,9... | collective-permute-start | bytes 884744 | tf_op jit(solution)/shard_map/ppermute | solution.py:14
  55.0 0.9 fusion.8
  55.9 3.0 %collective-permute-done.4 = f32[18,32,1,128]{3,1,2,0:T(8,128)S(1)} collective-permute-done((f32[18,32,1,128]{3,1,2,0:T(8,128)S(1)}, f32[18,32,1,128]{3,1,2,0:T(8,128)S(1)}, u32[]{:S(2)}, u32[]{:S(2)}) %collective-permute-start.4) | collective-permute-done | bytes 294944 | tf_op jit(solution)/shard_map/ppermute | solution.py:14
  58.9 1.9 %fusion.34 = f32[18,32,8,128]{3,1,2,0:T(8,128)S(1)} fusion(f32[18,32,7,128]{3,1,2,0:T(8,128)S(1)} %fusion.39, f32[18,32,1,128]{3,1,2,0:T(8,128)S(1)} %collective-permute-done.4, f32[18,32,8,127]{3,1,2,0:T(8,128)S(1)} %get-tuple-element.27, f32[18,32,8,127]{3,1,2,0:T(8,128)S(1)} %get-tuple-element.26, f32[9,32,8,128]{3,1,2,0:T(8,128)S(1)} %get-tuple-element.14, ...), kind=kLoop, calls=%fused_computation.65 | loop fusion | flops 8257536 | bytes 11768832 | tf_op jit(solution)/shard_map/add | solution.py:42
  60.8 0.2 fusion.61
  61.0 1.8 %fusion.38 = f32[18,32,8,128]{3,1,2,0:T(8,128)S(1)} fusion(f32[18,32,1,128]{3,1,2,0:T(8,128)S(1)} %collective-permute-done.5, f32[18,32,7,128]{3,1,2,0:T(8,128)S(1)} %slice.267, f32[18,32,8,127]{3,1,2,0:T(8,128)S(1)} %get-tuple-element.13, f32[18,32,8,127]{3,1,2,0:T(8,128)S(1)} %get-tuple-element.12, f32[36,32,8,128]{3,1,2,0:T(8,128)S(1)} %multiply_divide_fusion.1, ...), kind=kLoop, calls=%fused_computation.70 | loop fusion | flops 7667712 | bytes 11768832 | tf_op jit(solution)/shard_map/add | solution.py:42
  62.8 0.6 fusion.41
  63.4 0.1 multiply_add_fusion.1
  63.5 1.8 %fusion.4 = (f32[36,32,8,128]{3,1,2,0:T(8,128)S(1)}, f32[36,32,8,128]{3,1,2,0:T(8,128)S(1)}) fusion(f32[32]{0:T(128)S(1)} %power_multiply_fusion, f32[36,8,128]{2,1,0:T(8,128)S(1)} %multiply_add_fusion, f32[8,128]{1,0:T(8,128)S(1)} %convert_element_type.3, f32[9,32,8,128]{3,1,2,0:T(8,128)S(1)} %get-tuple-element.25, f32[18,32,8,128]{3,1,2,0:T(8,128)S(1)} %fusion.38, ...), kind=kLoop, calls=%fused_computation.12 | loop fusion | flops 12976128 | bytes 14438528 | tf_op jit(solution)/shard_map/mul | solution.py:59
  65.3 6.5 %copy.39 = f32[36,32,8,128]{3,2,1,0:T(8,128)} copy(f32[36,32,8,128]{3,1,2,0:T(8,128)S(1)} %get-tuple-element.11) | data formatting | bytes 9437184
  71.8 2.4 %fusion.45 = f32[2,8,128]{2,0,1:T(2,128)S(1)} fusion(f32[2,36,32,1]{2,0,1,3:T(2,128)S(1)} %copy.41, f32[36,32,8,128]{3,1,2,0:T(8,128)S(1)} %get-tuple-element.11), kind=kOutput, calls=%fused_computation.77 | convolution fusion | flops 28311552 | bytes 4736000 | tf_op jit(solution)/shard_map/cij,ijxy->cxy/dot_general | solution.py:64
  74.2 2.4 %fusion.42 = f32[2,8,128]{2,0,1:T(2,128)S(1)} fusion(f32[2,36,32,1]{2,0,1,3:T(2,128)S(1)} %copy.41, f32[36,32,8,128]{3,1,2,0:T(8,128)S(1)} %get-tuple-element.10), kind=kOutput, calls=%fused_computation.76 | convolution fusion | flops 28311552 | bytes 4736000 | tf_op jit(solution)/shard_map/cij,ijxy->cxy/dot_general | solution.py:63
  76.6 0.2 copy.37
  76.8 0.8 gather_fusion
  77.5 0.1 copy.38
  77.6 17.9 %all_gather.3 = f32[4,128,128]{1,0,2:T(4,128)S(1)} all-gather(f32[4,128,8]{1,0,2:T(4,128)S(1)} %copy.38), channel_id=1, replica_groups=mesh['member'=2,'gx'=16] {'gx'}, dimensions={2}, use_global_device_ids=true | all-gather | bytes 278528 | tf_op jit(solution)/shard_map/all_gather | solution.py:90
  95.5 0.2 constant_dynamic-slice_fusion
  95.7 0.7 copy.40
  (41 shorter events, 0.3 us)
Async XLA Ops:
  2.4 2.4 %copy-start = (f32[36,32,8,128]{3,2,1,0:T(8,128)S(1)}, f32[36,32,8,128]{3,2,1,0:T(8,128)}, u32[]{:S(2)}) copy-start(f32[36,32,8,128]{3,2,1,0:T(8,128)} %param.4) | copy-start | bytes 14155780
  3.6 18.8 %collective-permute-start = (f32[18,32,1,128]{3,1,2,0:T(8,128)}, f32[18,32,1,128]{3,1,2,0:T(8,128)S(1)}, u32[]{:S(2)}, u32[]{:S(2)}) collective-permute-start(f32[18,32,1,128]{3,1,2,0:T(8,128)} %slice.228), channel_id=1, source_target_pairs={{0,1},{1,2},{2,3},{3,4},{4,5},{5,6},{6,7},{7,8},{8,9},{9,10},{10,1... | collective-permute-start | bytes 884744 | tf_op jit(solution)/shard_map/ppermute | solution.py:14
  5.1 21.7 %collective-permute-start.1 = (f32[18,32,1,128]{3,1,2,0:T(8,128)S(1)}, f32[18,32,1,128]{3,1,2,0:T(8,128)S(1)}, u32[]{:S(2)}, u32[]{:S(2)}) collective-permute-start(f32[18,32,1,128]{3,1,2,0:T(8,128)S(1)} %bitcast.18), channel_id=1, source_target_pairs={{0,15},{1,0},{2,1},{3,2},{4,3},{5,4},{6,5},{7,6},{8,7},{9,8},{10,9... | collective-permute-start | bytes 884744 | tf_op jit(solution)/shard_map/ppermute | solution.py:14
  20.3 1.7 %copy-start.5 = (s32[8,128]{1,0:T(8,128)S(1)}, s32[8,128]{1,0:T(8,128)}, u32[]{:S(2)}) copy-start(s32[8,128]{1,0:T(8,128)} %param.6) | copy-start | bytes 12292
  20.3 1.7 %copy-start.4 = (f32[2,8,128]{2,1,0:T(8,128)S(1)}, f32[2,8,128]{2,1,0:T(8,128)}, u32[]{:S(2)}) copy-start(f32[2,8,128]{2,1,0:T(8,128)} %param.5) | copy-start | bytes 24580
  20.3 1.9 %copy-start.6 = (s32[128]{0:T(128)S(1)}, s32[128]{0:T(128)}, u32[]{:S(2)}) copy-start(s32[128]{0:T(128)} %param.7) | copy-start | bytes 1540
  22.4 4.3 %copy-start.2 = (f32[18,32,8,127]{3,1,2,0:T(8,128)S(1)}, f32[18,32,8,127]{3,1,2,0:T(8,128)}, u32[]{:S(2)}) copy-start(f32[18,32,8,127]{3,1,2,0:T(8,128)} %copy.59) | copy-start | bytes 7022596
  22.4 4.3 %copy-start.3 = (f32[18,32,7,128]{3,1,2,0:T(8,128)S(1)}, f32[18,32,7,128]{3,1,2,0:T(8,128)}, u32[]{:S(2)}) copy-start(f32[18,32,7,128]{3,1,2,0:T(8,128)} %copy.56) | copy-start | bytes 6193156
  26.4 1.7 %slice-start = ((f32[36,32,8,128]{3,2,1,0:T(8,128)}), f32[18,32,8,128]{3,2,1,0:T(8,128)S(1)}, s32[]{:S(2)}) async-start(f32[36,32,8,128]{3,2,1,0:T(8,128)} %param.4), calls=%async_computation | async-start | bytes 4718592 | tf_op jit(solution)/shard_map/slice | solution.py:79
  26.4 2.4 %copy-start.1 = (f32[18,32,8,127]{3,1,2,0:T(8,128)S(1)}, f32[18,32,8,127]{3,1,2,0:T(8,128)}, u32[]{:S(2)}) copy-start(f32[18,32,8,127]{3,1,2,0:T(8,128)} %copy.58) | copy-start | bytes 7022596
  33.8 8.9 %collective-permute-start.2 = (f32[18,32,1,128]{3,1,2,0:T(8,128)S(1)}, f32[18,32,1,128]{3,1,2,0:T(8,128)S(1)}, u32[]{:S(2)}, u32[]{:S(2)}) collective-permute-start(f32[18,32,1,128]{3,1,2,0:T(8,128)S(1)} %fusion.49), channel_id=1, source_target_pairs={{0,1},{1,2},{2,3},{3,4},{4,5},{5,6},{6,7},{7,8},{8,9},{9,10},{10,1... | collective-permute-start | bytes 884744 | tf_op jit(solution)/shard_map/ppermute | solution.py:14
  34.4 10.5 %collective-permute-start.3 = (f32[18,32,1,128]{3,1,2,0:T(8,128)S(1)}, f32[18,32,1,128]{3,1,2,0:T(8,128)S(1)}, u32[]{:S(2)}, u32[]{:S(2)}) collective-permute-start(f32[18,32,1,128]{3,1,2,0:T(8,128)S(1)} %slice.251), channel_id=1, source_target_pairs={{0,15},{1,0},{2,1},{3,2},{4,3},{5,4},{6,5},{7,6},{8,7},{9,8},{10,9... | collective-permute-start | bytes 884744 | tf_op jit(solution)/shard_map/ppermute | solution.py:14
  50.0 8.9 %collective-permute-start.4 = (f32[18,32,1,128]{3,1,2,0:T(8,128)S(1)}, f32[18,32,1,128]{3,1,2,0:T(8,128)S(1)}, u32[]{:S(2)}, u32[]{:S(2)}) collective-permute-start(f32[18,32,1,128]{3,1,2,0:T(8,128)S(1)} %fusion.48), channel_id=1, source_target_pairs={{0,1},{1,2},{2,3},{3,4},{4,5},{5,6},{6,7},{7,8},{8,9},{9,10},{10,1... | collective-permute-start | bytes 884744 | tf_op jit(solution)/shard_map/ppermute | solution.py:14
  50.5 10.5 %collective-permute-start.5 = (f32[18,32,1,128]{3,1,2,0:T(8,128)S(1)}, f32[18,32,1,128]{3,1,2,0:T(8,128)S(1)}, u32[]{:S(2)}, u32[]{:S(2)}) collective-permute-start(f32[18,32,1,128]{3,1,2,0:T(8,128)S(1)} %slice.268), channel_id=1, source_target_pairs={{0,15},{1,0},{2,1},{3,2},{4,3},{5,4},{6,5},{7,6},{8,7},{9,8},{10,9... | collective-permute-start | bytes 884744 | tf_op jit(solution)/shard_map/ppermute | solution.py:14
where the time goes:
time: 96.6 us; the launch traced here: 96.4 us
  local copies, waits for them, and re-layouts  29.2 us (30%)
  other arithmetic  22.3 us (23%)
  blocking collectives  17.9 us (19%)
  starting transfers between devices  15.3 us (16%)
  waiting for transfers between devices  5.77 us (6%)
  matrix products  4.79 us (5%)
  between operations  1.14 us (1%)
    all_gather x1, blocking collectives, per_device(): gathered = lax.all_gather(local_rows, 'gx', axis=2, tiled=True)  17.9 us
    ppermute x6, starting transfers between devices, passed_along(): return lax.ppermute(value, axis, pairs)  15.3 us
    unnamed x20, local copies, waits for them, and re-layouts  14.3 us
    add x6, other arithmetic, upwind(): center - jnp.maximum(along_x, 0.0) * (center - west_cell)  13.1 us
    ppermute x6, waiting for transfers between devices, passed_along(): return lax.ppermute(value, axis, pairs)  5.77 us
    slice x4, local copies, waits for them, and re-layouts, upwind(): south_cell = jnp.concatenate([border, center[..., :-1]], axis=3)  5.63 us
    div x2, other arithmetic, sources(): return (advected * (1.0 + growth) / (1.0 + damping), growth * advected)  2.77 us
    dot_general x1, matrix products, coupling_fields(): jnp.einsum('cij,ijxy->cxy', project, input_flux, precision=lax.Precision....  2.41 us
  transfers between devices with their start and end apart: 6, of which 2 were waited for; matrix products, arithmetic and copies ran while one was open for 24% of the time, Pallas kernels for 0%

commit v1 on v0

v1 whole, which is shorter than its diff:
```python
import functools
import math

import jax
import jax.numpy as jnp
import numpy as np
from jax import lax
from jax.experimental import pallas as pl
from jax.experimental.pallas import tpu as pltpu
from jax.sharding import PartitionSpec as P

STEPS = 3
SUB = 8
LEFT, RIGHT = 8, 10


def tables(directions, frequencies):
    angles = (np.arange(directions) + 0.5) * (2.0 * math.pi / directions)
    levels = np.arange(frequencies)
    shrink = 1.1 ** (-levels.astype(np.float64))
    inverse_speed = 2.0 * math.pi * (0.0418 / shrink) / 9.81
    weight = (levels + 1.0) / frequencies
    per_freq = np.stack([0.45 * shrink, inverse_speed, 0.3 * weight * weight,
                         weight * 3.0 / math.sqrt(directions * frequencies)])
    groups = frequencies // SUB
    per_freq = np.broadcast_to(per_freq.reshape(4, groups, SUB, 1), (4, groups, SUB, 128))
    return (np.stack([np.cos(angles), np.sin(angles)]).astype(np.float32),
            np.ascontiguousarray(per_freq).astype(np.float32))


def kernel(n, dirs, groups, trig, freq, spec, wind, land, bands, out, ocean,
           x_ref, w_ref, g_ref, send_e, send_w, halo_l, halo_r, wind_h, land_h,
           wind_b, mask_b, r_ref, e_send, e_halo, rows, sends, recv,
           in_sem, out_sem, ssem, rsem, a_ssem, a_rsem):
    me = lax.axis_index("gx")
    right, left = lax.rem(me + 1, n), lax.rem(me + n - 1, n)
    quarter = dirs // 4
    qrows = quarter * groups * SUB * SUB
    cells = dirs * groups * SUB
    lane = lax.broadcasted_iota(jnp.int32, (SUB, 128), 1)
    quads = [(q * quarter, q in (0, 3), q in (0, 1)) for q in range(4)]

    def in_copy(q):
        part = pl.ds(q * qrows, qrows)
        return pltpu.make_async_copy(spec.at[part], x_ref.at[part], in_sem.at[q])

    def out_copy(q):
        part = pl.ds(q * qrows, qrows)
        return pltpu.make_async_copy(x_ref.at[part], out.at[part], out_sem.at[q])

    for q in range(4):
        in_copy(q).start()

    barrier = pltpu.get_barrier_semaphore()

    def greet(i, _):
        pl.semaphore_signal(barrier, inc=1, device_id={"gx": lax.rem(me + i, n)},
                            device_id_type=pl.DeviceIdType.MESH)
        return 0

    lax.fori_loop(1, n, greet, 0)

    def remote(src, dst, slot, target):
        return pltpu.make_async_remote_copy(
            src_ref=src, dst_ref=dst, send_sem=ssem.at[slot], recv_sem=rsem.at[slot],
            device_id={"gx": target}, device_id_type=pl.DeviceIdType.MESH)

    bulk_e = [remote(send_e.at[k], halo_l.at[k], k, right) for k in range(3)]
    bulk_w = [remote(send_w.at[k], halo_r.at[k], 3 + k, left) for k in range(3)]
    small = [remote(wind, wind_h.at[0], 6, right), remote(wind, wind_h.at[1], 7, left),
             remote(land, land_h.at[0], 8, right), remote(land, land_h.at[1], 9, left)]
    energy_msg = [[remote(e_send.at[s], e_halo.at[s, 0], 10 + 2 * s, right),
                   remote(e_send.at[s], e_halo.at[s, 1], 11 + 2 * s, left)] for s in range(2)]

    for q, (d0, east, north) in enumerate(quads):
        in_copy(q).wait()
        base = d0 * groups
        local = (0 if q in (0, 1) else quarter) * groups

        def pack(i, _, base=base, local=local, east=east):
            for k in range(3):
                column = SUB - 1 - k if east else k
                value = x_ref[pl.ds((base + i) * SUB * SUB + column, SUB, stride=SUB), :]
                (send_e if east else send_w)[k, local + i] = value
            return 0

        lax.fori_loop(0, quarter * groups, pack, 0, unroll=4)

    def spread(slot, wind_tile, land_tile, column):
        for c in range(2):
            wind_b[c, slot] = jnp.broadcast_to(wind_tile[c][column:column + 1], (SUB, 128))
        mask_b[slot] = jnp.broadcast_to(
            land_tile[column:column + 1].astype(jnp.float32), (SUB, 128))

    own_wind = [wind[0], wind[1]]
    own_land = land[...]
    for x in range(SUB):
        spread(x, own_wind, own_land, x)

    pl.semaphore_wait(barrier, n - 1)
    for copy in small + [bulk_e[0], bulk_w[0], bulk_e[1], bulk_w[1]]:
        copy.start()

    def scalars(d):
        return trig[0, d], trig[1, d]

    def coefficients(cosine, sine, f, east, north):
        k = freq[0, f]
        along_x = k * (cosine if east else -cosine)
        along_y = k * (sine if north else -sine)
        centre = 1.0 - along_x - along_y
        return centre, along_x, jnp.where(lane == (0 if north else 127), 0.0, along_y)

    def shifted(value, north):
        return pltpu.roll(value, 1 if north else 127, 1)

    def growth_of(cosine, sine, f, slot):
        ratio = (wind_b[0, slot] * cosine + wind_b[1, slot] * sine) * freq[1, f]
        return 0.05 * jnp.minimum(jnp.maximum(ratio - 1.0, 0.0), 4.0)

    zero = jnp.zeros((SUB, 128), jnp.float32)

    def main(step, sums):
        for d0, east, north in quads:
            def body(i, sums, d0=d0, east=east, north=north):
                d = d0 + i
                cosine, sine = scalars(d)
                sums = list(sums)
                if step == 0:
                    speed = [wind_b[0, x] * cosine + wind_b[1, x] * sine for x in range(SUB)]
                for f in range(groups):
                    centre, along_x, along_y = coefficients(cosine, sine, f, east, north)
                    before = None
                    for x in (range(SUB) if east else range(SUB - 1, -1, -1)):
                        at = (d * groups + f) * SUB + x
                        if step == 0:
                            value = x_ref[pl.ds((d * groups + f) * SUB * SUB + x, SUB, stride=SUB), :]
                            g_ref[at] = 0.05 * jnp.minimum(
                                jnp.maximum(speed[x] * freq[1, f] - 1.0, 0.0), 4.0)
                        else:
                            value = w_ref[at] * (1.0 + g_ref[at]) * r_ref[x, f]
                        new = centre * value + along_y * shifted(value, north)
                        if before is not None:
                            new = new + along_x * before
                        before = value
                        w_ref[at] = new
                        sums[x] = sums[x] + new
                return tuple(sums)

            sums = lax.fori_loop(0, quarter, body, tuple(sums))
        return sums

    def fix(step, sums):
        first, last = sums[0], sums[SUB - 1]
        for q, (d0, east, north) in enumerate(quads):
            halo = halo_l if east else halo_r
            slot = LEFT if east else RIGHT
            edge = 0 if east else SUB - 1
            local = (0 if q in (0, 1) else quarter) * groups

            def body(i, total, d0=d0, east=east, north=north, halo=halo, slot=slot,
                     edge=edge, local=local):
                d = d0 + i
                cosine, sine = scalars(d)
                for f in range(groups):
                    centre, along_x, along_y = coefficients(cosine, sine, f, east, north)
                    at = local + i * groups + f

                    def advance(value, upwind, depth, s):
                        moved = centre * value + along_x * upwind + along_y * shifted(value, north)
                        growth = growth_of(cosine, sine, f, slot + depth)
                        return moved * (1.0 + growth) * r_ref[slot + depth + 4 * (s if depth == 0 else 0), f]

                    if step == 0:
                        flow = halo[0, at]
                    elif step == 1:
                        flow = advance(halo[0, at], halo[1, at], 0, 0)
                        halo[0, at] = flow
                    else:
                        far = advance(halo[1, at], halo[2, at], 1, 0)
                        flow = advance(halo[0, at], far, 0, 1)
                    extra = along_x * flow
                    cell = (d * groups + f) * SUB + edge
                    w_ref[cell] = w_ref[cell] + extra
                    total = total + extra
                return total

            if east:
                first = lax.fori_loop(0, quarter, body, first)
            else:
                last = lax.fori_loop(0, quarter, body, last)
        return (first,) + tuple(sums[1:-1]) + (last,)

    def energy_tile(sums):
        return jnp.concatenate(
            [jnp.sum(s * mask_b[x], axis=0, keepdims=True) for x, s in enumerate(sums)],
            axis=0) * (1.0 / cells)

    def factor(tile, column, mask_slot, slot):
        ratio = jnp.broadcast_to(tile[column:column + 1], (SUB, 128))
        for f in range(groups):
            r_ref[slot, f] = mask_b[mask_slot] / (1.0 + freq[2, f] * ratio)

    def own_factors(tile):
        ratio = tile / (0.5 + tile)
        for x in range(SUB):
            factor(ratio, x, x, x)

    sums = main(0, (zero,) * SUB)
    for copy in small:
        copy.wait()
    for side in range(2):
        tiles = [wind_h[side, 0], wind_h[side, 1]]
        land_tile = land_h[side]
        for depth in range(2):
            spread((LEFT if side == 0 else RIGHT) + depth, tiles, land_tile,
                   SUB - 1 - depth if side == 0 else depth)
    bulk_e[0].wait()
    bulk_w[0].wait()
    sums = fix(0, sums)
    for step in (1, 2):
        tile = energy_tile(sums)
        e_send[step - 1] = tile
        own_factors(tile)
        for copy in energy_msg[step - 1]:
            copy.start()
        if step == 1:
            bulk_e[2].start()
            bulk_w[2].start()
        sums = main(step, (zero,) * SUB)
        bulk_e[step].wait()
        bulk_w[step].wait()
        for copy in energy_msg[step - 1]:
            copy.wait()
        for side in range(2):
            seen = e_halo[step - 1, side]
            ratio = seen / (0.5 + seen)
            base = LEFT if side == 0 else RIGHT
            for depth in range(3 - step):
                factor(ratio, SUB - 1 - depth if side == 0 else depth, base + depth,
                       base + depth + 4 * (step - 1))
        sums = fix(step, sums)

    own_factors(energy_tile(sums))

    stress = [[zero] * SUB, [zero] * SUB]
    fields = [[None] * SUB for _ in range(4)]

    for q, (d0, east, north) in enumerate(quads):
        def body(i, carry, d0=d0):
            d = d0 + i
            cosine, sine = scalars(d)
            for x in range(SUB):
                flux, drift = zero, zero
                for f in range(groups):
                    at = (d * groups + f) * SUB + x
                    moved = w_ref[at]
                    flow = g_ref[at] * moved
                    after = (moved + flow) * r_ref[x, f]
                    x_ref[pl.ds((d * groups + f) * SUB * SUB + x, SUB, stride=SUB), :] = after
                    flux = flux + freq[3, f] * flow
                    drift = drift + freq[3, f] * after
                carry = list(carry)
                carry[x] = carry[x] + cosine * flux
                carry[SUB + x] = carry[SUB + x] + sine * flux
                carry[2 * SUB + x] = carry[2 * SUB + x] + cosine * drift
                carry[3 * SUB + x] = carry[3 * SUB + x] + sine * drift
            return tuple(carry)

        carry = lax.fori_loop(0, quarter, body, (zero,) * (4 * SUB) if q == 0 else carry)
        out_copy(q).start()

    total = []
    for j, value in enumerate(carry):
        if j < 2 * SUB:
            value = value * mask_b[j % SUB]
        total.append(jnp.sum(value, axis=0, keepdims=True))
    total.append(jnp.zeros((128 - 4 * SUB, 128), jnp.float32))
    stacked = jnp.concatenate(total, axis=0)
    lat = lax.broadcasted_iota(jnp.int32, (128, 128), 0)
    pick = (lat == bands[...]).astype(jnp.float32)
    picked = jnp.dot(stacked, pick, precision=lax.Precision.HIGHEST,
                     preferred_element_type=jnp.float32)
    rows[...] = picked.T
    band = 128 // n
    for k in range(n):
        sends[k] = rows[pl.ds(k * band, band), :]

    def exchange(i):
        target = lax.rem(me + i, n)
        return pltpu.make_async_remote_copy(
            src_ref=sends.at[target], dst_ref=recv.at[me], send_sem=a_ssem.at[i],
            recv_sem=a_rsem.at[i], device_id={"gx": target},
            device_id_type=pl.DeviceIdType.MESH)

    def begin(i, _):
        exchange(i).start()
        return 0

    def finish(i, _):
        exchange(i).wait()
        return 0

    lax.fori_loop(1, n, begin, 0)
    recv[pl.ds(me, 1)] = sends[pl.ds(me, 1)]
    lax.fori_loop(1, n, finish, 0)
    per_tile = 128 // SUB
    block = lax.broadcasted_iota(jnp.int32, (band, 128), 1) // SUB
    for tile in range(max(1, n // per_tile)):
        for c in range(4):
            built = jnp.zeros((band, 128), jnp.float32)
            for k in range(min(n, per_tile)):
                moved = pltpu.roll(recv[tile * per_tile + k], (SUB * (k - c)) % 128, 1)
                built = jnp.where(block == k, moved, built)
            ocean[c, :, tile * 128:(tile + 1) * 128] = built
    for q in range(4):
        out_copy(q).wait()


def per_device(n, spectrum, wind, land_sea, band_rows):
    dirs, freqs, columns, lats = spectrum.shape
    groups = freqs // SUB
    trig, freq = tables(dirs, freqs)
    half = dirs // 2 * groups
    band = lats // n
    f32 = jnp.float32
    vmem = pl.BlockSpec(memory_space=pltpu.VMEM)
    anywhere = pl.BlockSpec(memory_space=pl.ANY)
    cells = dirs * groups * SUB
    after, ocean = pl.pallas_call(
        functools.partial(kernel, n, dirs, groups),
        out_shape=(jax.ShapeDtypeStruct((cells * SUB, lats), f32),
                   jax.ShapeDtypeStruct((4, band, columns * n), f32)),
        in_specs=[pl.BlockSpec(memory_space=pltpu.SMEM), vmem, anywhere, vmem, vmem, vmem],
        out_specs=(anywhere, vmem),
        scratch_shapes=[
            pltpu.VMEM((cells * SUB, lats), f32),
            pltpu.VMEM((cells, SUB, lats), f32),
            pltpu.VMEM((cells, SUB, lats), f32),
            pltpu.VMEM((3, half, SUB, lats), f32),
            pltpu.VMEM((3, half, SUB, lats), f32),
            pltpu.VMEM((3, half, SUB, lats), f32),
            pltpu.VMEM((3, half, SUB, lats), f32),
            pltpu.VMEM((2, 2, SUB, lats), f32),
            pltpu.VMEM((2, SUB, lats), jnp.int32),
            pltpu.VMEM((2, 12, SUB, lats), f32),
            pltpu.VMEM((12, SUB, lats), f32),
            pltpu.VMEM((16, groups, SUB, lats), f32),
            pltpu.VMEM((2, SUB, lats), f32),
            pltpu.VMEM((2, 2, SUB, lats), f32),
            pltpu.VMEM((128, 128), f32),
            pltpu.VMEM((n, band, 128), f32),
            pltpu.VMEM((n, band, 128), f32),
            pltpu.SemaphoreType.DMA((4,)),
            pltpu.SemaphoreType.DMA((4,)),
            pltpu.SemaphoreType.DMA((14,)),
            pltpu.SemaphoreType.DMA((14,)),
            pltpu.SemaphoreType.DMA((n,)),
            pltpu.SemaphoreType.DMA((n,)),
        ],
        compiler_params=pltpu.CompilerParams(
            collective_id=0, has_side_effects=True, vmem_limit_bytes=48 * 2**20),
        name="wave_window",
    )(jnp.asarray(trig), jnp.asarray(freq), spectrum.reshape(cells * SUB, lats), wind, land_sea,
      band_rows.reshape(1, lats))
    return after.reshape(spectrum.shape), ocean


def solution(mesh):
    placed = (
        P(None, None, ("member", "gx"), None),
        P(None, ("member", "gx"), None),
        P("gx", None),
        P(),
    )
    return jax.shard_map(
        functools.partial(per_device, mesh.shape["gx"]),
        mesh=mesh,
        in_specs=placed,
        out_specs=(P(None, None, ("member", "gx"), None), P(None, "gx", "member")),
        check_vma=False,
    )
```

time: 96.6 us -> 50.6 us (0.52)
  Pallas kernels: 0 us -> 43.3 us
  local copies, waits for them, and re-layouts: 29.2 us -> 6.34 us
  other arithmetic: 22.3 us -> 0 us
  blocking collectives: 17.9 us -> 0 us
  starting transfers between devices: 15.3 us -> 0 us
  waiting for transfers between devices: 5.77 us -> 0 us
  matrix products: 4.79 us -> 0 us
    pallas_call x0 -> x1, Pallas kernels: none -> 43.3 us  [per_device(): pl.pallas_call(functools.partial(kernel, n, dirs, groups), out_shape=(jax...]
    all_gather x1 -> x0, blocking collectives: 17.9 us -> none  [per_device(): gathered = lax.all_gather(local_rows, 'gx', axis=2, tiled=True)]
    ppermute x6 -> x0, starting transfers between devices: 15.3 us -> none  [passed_along(): return lax.ppermute(value, axis, pairs)]
    add x10 -> x0, other arithmetic: 13.4 us -> none  [the longest x6 13.1 us: upwind(): center - jnp.maximum(along_x, 0.0) * (center - west_cell)]
    slice x22 -> x0, local copies, waits for them, and re-layouts: 13.4 us -> none  [the longest x4 5.63 us: upwind(): south_cell = jnp.concatenate([border, center[..., :-1]], axis=3)]
    unnamed x20 -> x12, local copies, waits for them, and re-layouts: 14.3 us -> 6.34 us
    ppermute x6 -> x0, waiting for transfers between devices: 5.77 us -> none  [passed_along(): return lax.ppermute(value, axis, pairs)]
    dot_general x2 -> x0, matrix products: 4.79 us -> none  [the longest x1 2.41 us: coupling_fields(): jnp.einsum('cij,ijxy->cxy', project, input_flux, precision=lax.Precision....]
  transfers between devices with their start and end apart: 6 -> 0, of which waited for: 2 -> 0; matrix products, arithmetic and copies ran while one was open for 24% -> 0% of each run, Pallas kernels for 0% -> 0%
where the time goes in v1:
time: 50.6 us; the launch traced here: 50.3 us
  Pallas kernels  43.3 us (86%)
  local copies, waits for them, and re-layouts  6.34 us (13%)
  between operations  0.65 us (1%)
    pallas_call x1, Pallas kernels, per_device(): pl.pallas_call(functools.partial(kernel, n, dirs, groups), out_shape=(jax...  43.3 us
    unnamed x12, local copies, waits for them, and re-layouts  6.34 us

profile of v1, /device:TPU:0, one launch (start us, length us, event | category | flops | bytes accessed | tf_op | source)
XLA Modules:
  0.0 50.3 jit_solution(4609240309698895394)
XLA Ops:
  0.6 0.0 copy-start
  0.6 0.8 %copy-done = f32[4,4,8,128]{3,2,1,0:T(8,128)S(1)} copy-done((f32[4,4,8,128]{3,2,1,0:T(8,128)S(1)}, f32[4,4,8,128]{3,2,1,0:T(8,128)}, u32[]{:S(2)}) %copy-start) | copy-done | bytes 65560
  1.5 0.0 copy-start.1
  1.5 0.7 %copy-done.1 = f32[2,8,128]{2,1,0:T(8,128)S(1)} copy-done((f32[2,8,128]{2,1,0:T(8,128)S(1)}, f32[2,8,128]{2,1,0:T(8,128)}, u32[]{:S(2)}) %copy-start.1) | copy-done | bytes 8216
  2.2 0.0 copy-start.2
  2.2 0.7 %copy-done.2 = s32[8,128]{1,0:T(8,128)S(1)} copy-done((s32[8,128]{1,0:T(8,128)S(1)}, s32[8,128]{1,0:T(8,128)}, u32[]{:S(2)}) %copy-start.2) | copy-done | bytes 4120
  2.9 0.0 copy-start.3
  2.9 0.7 %copy-done.3 = f32[2,36]{1,0:T(2,128)S(1)} copy-done((f32[2,36]{1,0:T(2,128)S(1)}, f32[2,36]{1,0:T(2,128)}, u32[]{:S(2)}) %copy-start.3) | copy-done | bytes 312
  3.5 0.0 copy-start.4
  3.5 0.7 %copy-done.4 = s32[128]{0:T(128)S(1)} copy-done((s32[128]{0:T(128)S(1)}, s32[128]{0:T(128)}, u32[]{:S(2)}) %copy-start.4) | copy-done | bytes 536
  4.2 43.3 %wave_window.1 = (f32[9216,128]{1,0:T(8,128)S(1)}, f32[4,8,128]{2,1,0:T(8,128)S(1)}) custom-call(f32[2,36]{1,0:T(2,128)S(1)} %copy-done.3, f32[4,4,8,128]{3,2,1,0:T(8,128)S(1)} %copy-done, f32[9216,128]{1,0:T(8,128)} %bitcast.5, f32[2,8,128]{2,1,0:T(8,128)S(1)} %copy-done.1, s32[8,128]{1,0:T(8,128)S(1)} %copy-done.2, s32[1,128]{1,0:T(1,128)S(1)} %bitcast.4), custom_call_target="tpu_custom_call" | custom-call | tf_op jit(solution)/shard_map/wave_window/pallas_call | solution.py:330
  47.5 2.2 %copy.10 = f32[36,32,8,128]{3,2,1,0:T(8,128)} copy(f32[36,32,8,128]{3,2,1,0:T(8,128)S(1)} %bitcast.3) | data formatting | bytes 9437184
  49.7 0.6 %copy.11 = f32[4,8,128]{2,1,0:T(8,128)} copy(f32[4,8,128]{2,1,0:T(8,128)S(1)} %get-tuple-element.9) | data formatting | bytes 32768
Async XLA Ops:
  0.6 0.8 %copy-start = (f32[4,4,8,128]{3,2,1,0:T(8,128)S(1)}, f32[4,4,8,128]{3,2,1,0:T(8,128)}, u32[]{:S(2)}) copy-start(f32[4,4,8,128]{3,2,1,0:T(8,128)} %constant.5.clone.freq) | copy-start | bytes 196612
  1.5 0.7 %copy-start.1 = (f32[2,8,128]{2,1,0:T(8,128)S(1)}, f32[2,8,128]{2,1,0:T(8,128)}, u32[]{:S(2)}) copy-start(f32[2,8,128]{2,1,0:T(8,128)} %wind.1) | copy-start | bytes 24580
  2.2 0.7 %copy-start.2 = (s32[8,128]{1,0:T(8,128)S(1)}, s32[8,128]{1,0:T(8,128)}, u32[]{:S(2)}) copy-start(s32[8,128]{1,0:T(8,128)} %land.1) | copy-start | bytes 12292
  2.9 0.7 %copy-start.3 = (f32[2,36]{1,0:T(2,128)S(1)}, f32[2,36]{1,0:T(2,128)}, u32[]{:S(2)}) copy-start(f32[2,36]{1,0:T(2,128)} %constant.4.clone.trig) | copy-start | bytes 868
  3.5 0.7 %copy-start.4 = (s32[128]{0:T(128)S(1)}, s32[128]{0:T(128)}, u32[]{:S(2)}) copy-start(s32[128]{0:T(128)} %param.9) | copy-start | bytes 1540

commit v2 on v1

--- a/solution.py
+++ b/solution.py
@@ -28,10 +28,10 @@
             np.ascontiguousarray(per_freq).astype(np.float32))
 
 
-def kernel(n, dirs, groups, trig, freq, spec, wind, land, bands, out, ocean,
-           x_ref, w_ref, g_ref, send_e, send_w, halo_l, halo_r, wind_h, land_h,
-           wind_b, mask_b, r_ref, e_send, e_halo, rows, sends, recv,
-           in_sem, out_sem, ssem, rsem, a_ssem, a_rsem):
+def kernel(n, dirs, groups, trig_in, freq_in, spec, wind_in, land_in, bands_in, out, ocean,
+           trig, freq, wind, land, bands, x_ref, w_ref, g_ref, send_e, send_w, halo_l, halo_r, wind_h, land_h,
+           wind_b, mask_b, r_ref, drift_ref, e_send, e_halo, rows, sends, recv,
+           in_sem, small_sem, ssem, rsem, a_ssem, a_rsem):
     me = lax.axis_index("gx")
     right, left = lax.rem(me + 1, n), lax.rem(me + n - 1, n)
     quarter = dirs // 4
@@ -44,10 +44,10 @@
         part = pl.ds(q * qrows, qrows)
         return pltpu.make_async_copy(spec.at[part], x_ref.at[part], in_sem.at[q])
 
-    def out_copy(q):
-        part = pl.ds(q * qrows, qrows)
-        return pltpu.make_async_copy(x_ref.at[part], out.at[part], out_sem.at[q])
-
+    tables_in = [pltpu.make_async_copy(src, dst, small_sem.at[i]) for i, (src, dst) in enumerate(
+        [(trig_in, trig), (freq_in, freq), (wind_in, wind), (land_in, land), (bands_in, bands)])]
+    for copy in tables_in:
+        copy.start()
     for q in range(4):
         in_copy(q).start()
 
@@ -85,6 +85,9 @@
             return 0
 
         lax.fori_loop(0, quarter * groups, pack, 0, unroll=4)
+
+    for copy in tables_in:
+        copy.wait()
 
     def spread(slot, wind_tile, land_tile, column):
         for c in range(2):
@@ -243,32 +246,27 @@
 
     own_factors(energy_tile(sums))
 
-    stress = [[zero] * SUB, [zero] * SUB]
-    fields = [[None] * SUB for _ in range(4)]
-
-    for q, (d0, east, north) in enumerate(quads):
-        def body(i, carry, d0=d0):
-            d = d0 + i
-            cosine, sine = scalars(d)
-            for x in range(SUB):
-                flux, drift = zero, zero
-                for f in range(groups):
-                    at = (d * groups + f) * SUB + x
-                    moved = w_ref[at]
-                    flow = g_ref[at] * moved
-                    after = (moved + flow) * r_ref[x, f]
-                    x_ref[pl.ds((d * groups + f) * SUB * SUB + x, SUB, stride=SUB), :] = after
-                    flux = flux + freq[3, f] * flow
-                    drift = drift + freq[3, f] * after
-                carry = list(carry)
-                carry[x] = carry[x] + cosine * flux
-                carry[SUB + x] = carry[SUB + x] + sine * flux
-                carry[2 * SUB + x] = carry[2 * SUB + x] + cosine * drift
-                carry[3 * SUB + x] = carry[3 * SUB + x] + sine * drift
-            return tuple(carry)
-
-        carry = lax.fori_loop(0, quarter, body, (zero,) * (4 * SUB) if q == 0 else carry)
-        out_copy(q).start()
+    def gather(d, carry):
+        cosine, sine = scalars(d)
+        carry = list(carry)
+        for x in range(SUB):
+            flux, drift = zero, zero
+            for f in range(groups):
+                at = (d * groups + f) * SUB + x
+                moved = w_ref[at]
+                flow = g_ref[at] * moved
+                flux = flux + freq[3, f] * flow
+                drift = drift + drift_ref[x, f] * (moved + flow)
+            carry[x] = carry[x] + cosine * flux
+            carry[SUB + x] = carry[SUB + x] + sine * flux
+            carry[2 * SUB + x] = carry[2 * SUB + x] + cosine * drift
+            carry[3 * SUB + x] = carry[3 * SUB + x] + sine * drift
+        return tuple(carry)
+
+    for x in range(SUB):
+        for f in range(groups):
+            drift_ref[x, f] = freq[3, f] * r_ref[x, f]
+    carry = lax.fori_loop(0, dirs, gather, (zero,) * (4 * SUB))
 
     total = []
     for j, value in enumerate(carry):
@@ -303,6 +301,17 @@
 
     lax.fori_loop(1, n, begin, 0)
     recv[pl.ds(me, 1)] = sends[pl.ds(me, 1)]
+
+    def write(d, _):
+        for f in range(groups):
+            for x in range(SUB):
+                at = (d * groups + f) * SUB + x
+                moved = w_ref[at]
+                out[pl.ds((d * groups + f) * SUB * SUB + x, SUB, stride=SUB), :] = (
+                    moved * (1.0 + g_ref[at]) * r_ref[x, f])
+        return 0
+
+    lax.fori_loop(0, dirs, write, 0)
     lax.fori_loop(1, n, finish, 0)
     per_tile = 128 // SUB
     block = lax.broadcasted_iota(jnp.int32, (band, 128), 1) // SUB
@@ -313,8 +322,6 @@
                 moved = pltpu.roll(recv[tile * per_tile + k], (SUB * (k - c)) % 128, 1)
                 built = jnp.where(block == k, moved, built)
             ocean[c, :, tile * 128:(tile + 1) * 128] = built
-    for q in range(4):
-        out_copy(q).wait()
 
 
 def per_device(n, spectrum, wind, land_sea, band_rows):
@@ -325,15 +332,20 @@
     band = lats // n
     f32 = jnp.float32
     vmem = pl.BlockSpec(memory_space=pltpu.VMEM)
-    anywhere = pl.BlockSpec(memory_space=pl.ANY)
+    anywhere = pl.BlockSpec(memory_space=pltpu.HBM)
     cells = dirs * groups * SUB
     after, ocean = pl.pallas_call(
         functools.partial(kernel, n, dirs, groups),
         out_shape=(jax.ShapeDtypeStruct((cells * SUB, lats), f32),
                    jax.ShapeDtypeStruct((4, band, columns * n), f32)),
-        in_specs=[pl.BlockSpec(memory_space=pltpu.SMEM), vmem, anywhere, vmem, vmem, vmem],
-        out_specs=(anywhere, vmem),
+        in_specs=[anywhere] * 6,
+        out_specs=(vmem, vmem),
         scratch_shapes=[
+            pltpu.SMEM(trig.shape, f32),
+            pltpu.VMEM(freq.shape, f32),
+            pltpu.VMEM((2, SUB, lats), f32),
+            pltpu.VMEM((SUB, lats), jnp.int32),
+            pltpu.VMEM((1, lats), jnp.int32),
             pltpu.VMEM((cells * SUB, lats), f32),
             pltpu.VMEM((cells, SUB, lats), f32),
             pltpu.VMEM((cells, SUB, lats), f32),
@@ -346,13 +358,14 @@
             pltpu.VMEM((2, 12, SUB, lats), f32),
             pltpu.VMEM((12, SUB, lats), f32),
             pltpu.VMEM((16, groups, SUB, lats), f32),
+            pltpu.VMEM((SUB, groups, SUB, lats), f32),
             pltpu.VMEM((2, SUB, lats), f32),
             pltpu.VMEM((2, 2, SUB, lats), f32),
             pltpu.VMEM((128, 128), f32),
             pltpu.VMEM((n, band, 128), f32),
             pltpu.VMEM((n, band, 128), f32),
             pltpu.SemaphoreType.DMA((4,)),
-            pltpu.SemaphoreType.DMA((4,)),
+            pltpu.SemaphoreType.DMA((5,)),
             pltpu.SemaphoreType.DMA((14,)),
             pltpu.SemaphoreType.DMA((14,)),
             pltpu.SemaphoreType.DMA((n,)),

time: 50.6 us -> 49 us (0.968)
  Pallas kernels: 43.3 us -> 41.7 us
    pallas_call x1, Pallas kernels: 43.3 us -> 41.7 us  [per_device(): pl.pallas_call(functools.partial(kernel, n, dirs, groups), out_shape=(jax...]
where the time goes in v2:
time: 49 us; the launch traced here: 48.7 us
  Pallas kernels  41.7 us (85%)
  local copies, waits for them, and re-layouts  6.34 us (13%)
  between operations  0.65 us (1%)
    pallas_call x1, Pallas kernels, per_device(): pl.pallas_call(functools.partial(kernel, n, dirs, groups), out_shape=(jax...  41.7 us
    unnamed x12, local copies, waits for them, and re-layouts  6.34 us

profile of v2, /device:TPU:0, one launch (start us, length us, event | category | flops | bytes accessed | tf_op | source)
XLA Modules:
  0.0 48.7 jit_solution(9874151552413843527)
XLA Ops:
  0.6 0.0 copy-start
  0.6 0.8 %copy-done = f32[4,4,8,128]{3,2,1,0:T(8,128)S(1)} copy-done((f32[4,4,8,128]{3,2,1,0:T(8,128)S(1)}, f32[4,4,8,128]{3,2,1,0:T(8,128)}, u32[]{:S(2)}) %copy-start) | copy-done | bytes 65560
  1.5 0.0 copy-start.1
  1.5 0.7 %copy-done.1 = f32[2,8,128]{2,1,0:T(8,128)S(1)} copy-done((f32[2,8,128]{2,1,0:T(8,128)S(1)}, f32[2,8,128]{2,1,0:T(8,128)}, u32[]{:S(2)}) %copy-start.1) | copy-done | bytes 8216
  2.2 0.0 copy-start.2
  2.2 0.7 %copy-done.2 = s32[8,128]{1,0:T(8,128)S(1)} copy-done((s32[8,128]{1,0:T(8,128)S(1)}, s32[8,128]{1,0:T(8,128)}, u32[]{:S(2)}) %copy-start.2) | copy-done | bytes 4120
  2.9 0.0 copy-start.3
  2.9 0.7 %copy-done.3 = f32[2,36]{1,0:T(2,128)S(1)} copy-done((f32[2,36]{1,0:T(2,128)S(1)}, f32[2,36]{1,0:T(2,128)}, u32[]{:S(2)}) %copy-start.3) | copy-done | bytes 312
  3.5 0.0 copy-start.4
  3.5 0.7 %copy-done.4 = s32[128]{0:T(128)S(1)} copy-done((s32[128]{0:T(128)S(1)}, s32[128]{0:T(128)}, u32[]{:S(2)}) %copy-start.4) | copy-done | bytes 536
  4.2 41.7 %wave_window.1 = (f32[9216,128]{1,0:T(8,128)S(1)}, f32[4,8,128]{2,1,0:T(8,128)S(1)}) custom-call(f32[2,36]{1,0:T(2,128)S(1)} %copy-done.3, f32[4,4,8,128]{3,2,1,0:T(8,128)S(1)} %copy-done, f32[9216,128]{1,0:T(8,128)} %bitcast.5, f32[2,8,128]{2,1,0:T(8,128)S(1)} %copy-done.1, s32[8,128]{1,0:T(8,128)S(1)} %copy-done.2, s32[1,128]{1,0:T(1,128)S(1)} %bitcast.4), custom_call_target="tpu_custom_call" | custom-call | tf_op jit(solution)/shard_map/wave_window/pallas_call | solution.py:337
  45.9 2.2 %copy.10 = f32[36,32,8,128]{3,2,1,0:T(8,128)} copy(f32[36,32,8,128]{3,2,1,0:T(8,128)S(1)} %bitcast.3) | data formatting | bytes 9437184
  48.1 0.6 %copy.11 = f32[4,8,128]{2,1,0:T(8,128)} copy(f32[4,8,128]{2,1,0:T(8,128)S(1)} %get-tuple-element.9) | data formatting | bytes 32768
Async XLA Ops:
  0.6 0.8 %copy-start = (f32[4,4,8,128]{3,2,1,0:T(8,128)S(1)}, f32[4,4,8,128]{3,2,1,0:T(8,128)}, u32[]{:S(2)}) copy-start(f32[4,4,8,128]{3,2,1,0:T(8,128)} %constant.5.clone.freq_in) | copy-start | bytes 196612
  1.5 0.7 %copy-start.1 = (f32[2,8,128]{2,1,0:T(8,128)S(1)}, f32[2,8,128]{2,1,0:T(8,128)}, u32[]{:S(2)}) copy-start(f32[2,8,128]{2,1,0:T(8,128)} %wind_in.1) | copy-start | bytes 24580
  2.2 0.7 %copy-start.2 = (s32[8,128]{1,0:T(8,128)S(1)}, s32[8,128]{1,0:T(8,128)}, u32[]{:S(2)}) copy-start(s32[8,128]{1,0:T(8,128)} %land_in.1) | copy-start | bytes 12292
  2.9 0.7 %copy-start.3 = (f32[2,36]{1,0:T(2,128)S(1)}, f32[2,36]{1,0:T(2,128)}, u32[]{:S(2)}) copy-start(f32[2,36]{1,0:T(2,128)} %constant.4.clone.trig_in) | copy-start | bytes 868
  3.5 0.7 %copy-start.4 = (s32[128]{0:T(128)S(1)}, s32[128]{0:T(128)}, u32[]{:S(2)}) copy-start(s32[128]{0:T(128)} %param.9) | copy-start | bytes 1540

commit v3 on v2

--- a/solution.py
+++ b/solution.py
@@ -3,7 +3,6 @@
 
 import jax
 import jax.numpy as jnp
-import numpy as np
 from jax import lax
 from jax.experimental import pallas as pl
 from jax.experimental.pallas import tpu as pltpu
@@ -14,21 +13,7 @@
 LEFT, RIGHT = 8, 10
 
 
-def tables(directions, frequencies):
-    angles = (np.arange(directions) + 0.5) * (2.0 * math.pi / directions)
-    levels = np.arange(frequencies)
-    shrink = 1.1 ** (-levels.astype(np.float64))
-    inverse_speed = 2.0 * math.pi * (0.0418 / shrink) / 9.81
-    weight = (levels + 1.0) / frequencies
-    per_freq = np.stack([0.45 * shrink, inverse_speed, 0.3 * weight * weight,
-                         weight * 3.0 / math.sqrt(directions * frequencies)])
-    groups = frequencies // SUB
-    per_freq = np.broadcast_to(per_freq.reshape(4, groups, SUB, 1), (4, groups, SUB, 128))
-    return (np.stack([np.cos(angles), np.sin(angles)]).astype(np.float32),
-            np.ascontiguousarray(per_freq).astype(np.float32))
-
-
-def kernel(n, dirs, groups, trig_in, freq_in, spec, wind_in, land_in, bands_in, out, ocean,
+def kernel(n, dirs, groups, spec, wind_in, land_in, bands_in, out, ocean,
            trig, freq, wind, land, bands, x_ref, w_ref, g_ref, send_e, send_w, halo_l, halo_r, wind_h, land_h,
            wind_b, mask_b, r_ref, drift_ref, e_send, e_halo, rows, sends, recv,
            in_sem, small_sem, ssem, rsem, a_ssem, a_rsem):
@@ -45,11 +30,25 @@
         return pltpu.make_async_copy(spec.at[part], x_ref.at[part], in_sem.at[q])
 
     tables_in = [pltpu.make_async_copy(src, dst, small_sem.at[i]) for i, (src, dst) in enumerate(
-        [(trig_in, trig), (freq_in, freq), (wind_in, wind), (land_in, land), (bands_in, bands)])]
+        [(wind_in, wind), (land_in, land), (bands_in, bands)])]
     for copy in tables_in:
         copy.start()
     for q in range(4):
         in_copy(q).start()
+
+    for d in range(dirs):
+        angle = (d + 0.5) * (2.0 * math.pi / dirs)
+        trig[0, d] = jnp.float32(math.cos(angle))
+        trig[1, d] = jnp.float32(math.sin(angle))
+    freqs = groups * SUB
+    for f in range(groups):
+        level = (lax.broadcasted_iota(jnp.int32, (SUB, 128), 0) + f * SUB).astype(jnp.float32)
+        weight = (level + 1.0) * (1.0 / freqs)
+        grown = jnp.exp(level * math.log(1.1))
+        freq[0, f] = 0.45 / grown
+        freq[1, f] = grown * (2.0 * math.pi * 0.0418 / 9.81)
+        freq[2, f] = 0.3 * weight * weight
+        freq[3, f] = weight * (3.0 / math.sqrt(dirs * freqs))
 
     barrier = pltpu.get_barrier_semaphore()
 
@@ -107,15 +106,17 @@
     def scalars(d):
         return trig[0, d], trig[1, d]
 
-    def coefficients(cosine, sine, f, east, north):
+    halves = [(0, 2 * quarter, True), (quarter, 0, False)]
+
+    def coefficients(cosine, sine, f, east, turn):
         k = freq[0, f]
         along_x = k * (cosine if east else -cosine)
-        along_y = k * (sine if north else -sine)
+        along_y = k * jnp.abs(sine)
         centre = 1.0 - along_x - along_y
-        return centre, along_x, jnp.where(lane == (0 if north else 127), 0.0, along_y)
-
-    def shifted(value, north):
-        return pltpu.roll(value, 1 if north else 127, 1)
+        return centre, along_x, jnp.where(lane == 127 * turn, 0.0, along_y)
+
+    def shifted(value, turn):
+        return pltpu.roll(value, 1 + 126 * turn, 1)
 
     def growth_of(cosine, sine, f, slot):
         ratio = (wind_b[0, slot] * cosine + wind_b[1, slot] * sine) * freq[1, f]
@@ -124,15 +125,16 @@
     zero = jnp.zeros((SUB, 128), jnp.float32)
 
     def main(step, sums):
-        for d0, east, north in quads:
-            def body(i, sums, d0=d0, east=east, north=north):
-                d = d0 + i
+        for d0, skip, east in halves:
+            def body(i, sums, d0=d0, skip=skip, east=east):
+                turn = i // quarter
+                d = d0 + i + skip * turn
                 cosine, sine = scalars(d)
                 sums = list(sums)
                 if step == 0:
                     speed = [wind_b[0, x] * cosine + wind_b[1, x] * sine for x in range(SUB)]
                 for f in range(groups):
-                    centre, along_x, along_y = coefficients(cosine, sine, f, east, north)
+                    centre, along_x, along_y = coefficients(cosine, sine, f, east, turn)
                     before = None
                     for x in (range(SUB) if east else range(SUB - 1, -1, -1)):
                         at = (d * groups + f) * SUB + x
@@ -142,7 +144,7 @@
                                 jnp.maximum(speed[x] * freq[1, f] - 1.0, 0.0), 4.0)
                         else:
                             value = w_ref[at] * (1.0 + g_ref[at]) * r_ref[x, f]
-                        new = centre * value + along_y * shifted(value, north)
+                        new = centre * value + along_y * shifted(value, turn)
                         if before is not None:
                             new = new + along_x * before
                         before = value
@@ -150,27 +152,26 @@
                         sums[x] = sums[x] + new
                 return tuple(sums)
 
-            sums = lax.fori_loop(0, quarter, body, tuple(sums))
+            sums = lax.fori_loop(0, 2 * quarter, body, tuple(sums))
         return sums
 
     def fix(step, sums):
         first, last = sums[0], sums[SUB - 1]
-        for q, (d0, east, north) in enumerate(quads):
+        for d0, skip, east in halves:
             halo = halo_l if east else halo_r
             slot = LEFT if east else RIGHT
             edge = 0 if east else SUB - 1
-            local = (0 if q in (0, 1) else quarter) * groups
-
-            def body(i, total, d0=d0, east=east, north=north, halo=halo, slot=slot,
-                     edge=edge, local=local):
-                d = d0 + i
+
+            def body(i, total, d0=d0, skip=skip, east=east, halo=halo, slot=slot, edge=edge):
+                turn = i // quarter
+                d = d0 + i + skip * turn
                 cosine, sine = scalars(d)
                 for f in range(groups):
-                    centre, along_x, along_y = coefficients(cosine, sine, f, east, north)
-                    at = local + i * groups + f
+                    centre, along_x, along_y = coefficients(cosine, sine, f, east, turn)
+                    at = i * groups + f
 
                     def advance(value, upwind, depth, s):
-                        moved = centre * value + along_x * upwind + along_y * shifted(value, north)
+                        moved = centre * value + along_x * upwind + along_y * shifted(value, turn)
                         growth = growth_of(cosine, sine, f, slot + depth)
                         return moved * (1.0 + growth) * r_ref[slot + depth + 4 * (s if depth == 0 else 0), f]
 
@@ -189,9 +190,9 @@
                 return total
 
             if east:
-                first = lax.fori_loop(0, quarter, body, first)
+                first = lax.fori_loop(0, 2 * quarter, body, first)
             else:
-                last = lax.fori_loop(0, quarter, body, last)
+                last = lax.fori_loop(0, 2 * quarter, body, last)
         return (first,) + tuple(sums[1:-1]) + (last,)
 
     def energy_tile(sums):
@@ -327,7 +328,6 @@
 def per_device(n, spectrum, wind, land_sea, band_rows):
     dirs, freqs, columns, lats = spectrum.shape
     groups = freqs // SUB
-    trig, freq = tables(dirs, freqs)
     half = dirs // 2 * groups
     band = lats // n
     f32 = jnp.float32
@@ -338,11 +338,11 @@
         functools.partial(kernel, n, dirs, groups),
         out_shape=(jax.ShapeDtypeStruct((cells * SUB, lats), f32),
                    jax.ShapeDtypeStruct((4, band, columns * n), f32)),
-        in_specs=[anywhere] * 6,
+        in_specs=[anywhere] * 4,
         out_specs=(vmem, vmem),
         scratch_shapes=[
-            pltpu.SMEM(trig.shape, f32),
-            pltpu.VMEM(freq.shape, f32),
+            pltpu.SMEM((2, dirs), f32),
+            pltpu.VMEM((4, groups, SUB, lats), f32),
             pltpu.VMEM((2, SUB, lats), f32),
             pltpu.VMEM((SUB, lats), jnp.int32),
             pltpu.VMEM((1, lats), jnp.int32),
@@ -365,7 +365,7 @@
             pltpu.VMEM((n, band, 128), f32),
             pltpu.VMEM((n, band, 128), f32),
             pltpu.SemaphoreType.DMA((4,)),
-            pltpu.SemaphoreType.DMA((5,)),
+            pltpu.SemaphoreType.DMA((3,)),
             pltpu.SemaphoreType.DMA((14,)),
             pltpu.SemaphoreType.DMA((14,)),
             pltpu.SemaphoreType.DMA((n,)),
@@ -374,7 +374,7 @@
         compiler_params=pltpu.CompilerParams(
             collective_id=0, has_side_effects=True, vmem_limit_bytes=48 * 2**20),
         name="wave_window",
-    )(jnp.asarray(trig), jnp.asarray(freq), spectrum.reshape(cells * SUB, lats), wind, land_sea,
+    )(spectrum.reshape(cells * SUB, lats), wind, land_sea,
       band_rows.reshape(1, lats))
     return after.reshape(spectrum.shape), ocean
 

time: 49 us -> 48.2 us (0.984)
  local copies, waits for them, and re-layouts: 6.34 us -> 4.82 us
  Pallas kernels: 41.7 us -> 42.4 us
    unnamed x12 -> x8, local copies, waits for them, and re-layouts: 6.34 us -> 4.82 us
    pallas_call x1, Pallas kernels: 41.7 us -> 42.4 us  [per_device(): pl.pallas_call(functools.partial(kernel, n, dirs, groups), out_shape=(jax...]
where the time goes in v3:
time: 48.2 us; the launch traced here: 47.9 us
  Pallas kernels  42.4 us (88%)
  local copies, waits for them, and re-layouts  4.82 us (10%)
  between operations  0.65 us (1%)
    pallas_call x1, Pallas kernels, per_device(): pl.pallas_call(functools.partial(kernel, n, dirs, groups), out_shape=(jax...  42.4 us
    unnamed x8, local copies, waits for them, and re-layouts  4.82 us

profile of v3, /device:TPU:0, one launch (start us, length us, event | category | flops | bytes accessed | tf_op | source)
XLA Modules:
  0.0 47.9 jit_solution(13610723385946712579)
XLA Ops:
  0.6 0.0 copy-start
  0.6 0.7 %copy-done = f32[2,8,128]{2,1,0:T(8,128)S(1)} copy-done((f32[2,8,128]{2,1,0:T(8,128)S(1)}, f32[2,8,128]{2,1,0:T(8,128)}, u32[]{:S(2)}) %copy-start) | copy-done | bytes 8216
  1.3 0.0 copy-start.1
  1.3 0.7 %copy-done.1 = s32[8,128]{1,0:T(8,128)S(1)} copy-done((s32[8,128]{1,0:T(8,128)S(1)}, s32[8,128]{1,0:T(8,128)}, u32[]{:S(2)}) %copy-start.1) | copy-done | bytes 4120
  2.0 0.0 copy-start.2
  2.0 0.7 %copy-done.2 = s32[128]{0:T(128)S(1)} copy-done((s32[128]{0:T(128)S(1)}, s32[128]{0:T(128)}, u32[]{:S(2)}) %copy-start.2) | copy-done | bytes 536
  2.7 42.4 %wave_window.1 = (f32[9216,128]{1,0:T(8,128)S(1)}, f32[4,8,128]{2,1,0:T(8,128)S(1)}) custom-call(f32[9216,128]{1,0:T(8,128)} %bitcast.5, f32[2,8,128]{2,1,0:T(8,128)S(1)} %copy-done, s32[8,128]{1,0:T(8,128)S(1)} %copy-done.1, s32[1,128]{1,0:T(1,128)S(1)} %bitcast.4), custom_call_target="tpu_custom_call" | custom-call | tf_op jit(solution)/shard_map/wave_window/pallas_call | solution.py:337
  45.1 2.2 %copy.8 = f32[36,32,8,128]{3,2,1,0:T(8,128)} copy(f32[36,32,8,128]{3,2,1,0:T(8,128)S(1)} %bitcast.3) | data formatting | bytes 9437184
  47.3 0.6 %copy.9 = f32[4,8,128]{2,1,0:T(8,128)} copy(f32[4,8,128]{2,1,0:T(8,128)S(1)} %get-tuple-element.9) | data formatting | bytes 32768
Async XLA Ops:
  0.6 0.7 %copy-start = (f32[2,8,128]{2,1,0:T(8,128)S(1)}, f32[2,8,128]{2,1,0:T(8,128)}, u32[]{:S(2)}) copy-start(f32[2,8,128]{2,1,0:T(8,128)} %wind_in.1) | copy-start | bytes 24580
  1.3 0.7 %copy-start.1 = (s32[8,128]{1,0:T(8,128)S(1)}, s32[8,128]{1,0:T(8,128)}, u32[]{:S(2)}) copy-start(s32[8,128]{1,0:T(8,128)} %land_in.1) | copy-start | bytes 12292
  2.0 0.7 %copy-start.2 = (s32[128]{0:T(128)S(1)}, s32[128]{0:T(128)}, u32[]{:S(2)}) copy-start(s32[128]{0:T(128)} %param.7) | copy-start | bytes 1540

commit v4 on v3

--- a/solution.py
+++ b/solution.py
@@ -15,7 +15,7 @@
 
 def kernel(n, dirs, groups, spec, wind_in, land_in, bands_in, out, ocean,
            trig, freq, wind, land, bands, x_ref, w_ref, g_ref, send_e, send_w, halo_l, halo_r, wind_h, land_h,
-           wind_b, mask_b, r_ref, drift_ref, e_send, e_halo, rows, sends, recv,
+           wind_b, mask_b, r_ref, acc, e_send, e_halo, rows, sends, recv,
            in_sem, small_sem, ssem, rsem, a_ssem, a_rsem):
     me = lax.axis_index("gx")
     right, left = lax.rem(me + 1, n), lax.rem(me + n - 1, n)
@@ -187,6 +187,10 @@
                     cell = (d * groups + f) * SUB + edge
                     w_ref[cell] = w_ref[cell] + extra
                     total = total + extra
+                    if step == STEPS - 1:
+                        flux = g_ref[cell] * extra
+                        for c, part in enumerate((flux, flux, extra + flux, extra + flux)):
+                            acc[c, edge, f] = acc[c, edge, f] + (sine if c % 2 else cosine) * part
                 return total
 
             if east:
@@ -194,6 +198,25 @@
             else:
                 last = lax.fori_loop(0, 2 * quarter, body, last)
         return (first,) + tuple(sums[1:-1]) + (last,)
+
+    def gather():
+        for f in range(groups):
+            def body(d, carry, f=f):
+                cosine, sine = scalars(d)
+                carry = list(carry)
+                for x in range(SUB):
+                    at = (d * groups + f) * SUB + x
+                    moved = w_ref[at]
+                    flux = g_ref[at] * moved
+                    after = moved + flux
+                    for c, part in enumerate((flux, flux, after, after)):
+                        carry[c * SUB + x] = carry[c * SUB + x] + (sine if c % 2 else cosine) * part
+                return tuple(carry)
+
+            carry = lax.fori_loop(0, dirs, body, (zero,) * (4 * SUB))
+            for c in range(4):
+                for x in range(SUB):
+                    acc[c, x, f] = carry[c * SUB + x]
 
     def energy_tile(sums):
         return jnp.concatenate(
@@ -232,6 +255,8 @@
             bulk_e[2].start()
             bulk_w[2].start()
         sums = main(step, (zero,) * SUB)
+        if step == STEPS - 1:
+            gather()
         bulk_e[step].wait()
         bulk_w[step].wait()
         for copy in energy_msg[step - 1]:
@@ -247,33 +272,14 @@
 
     own_factors(energy_tile(sums))
 
-    def gather(d, carry):
-        cosine, sine = scalars(d)
-        carry = list(carry)
+    total = []
+    for c in range(4):
         for x in range(SUB):
-            flux, drift = zero, zero
+            value = zero
             for f in range(groups):
-                at = (d * groups + f) * SUB + x
-                moved = w_ref[at]
-                flow = g_ref[at] * moved
-                flux = flux + freq[3, f] * flow
-                drift = drift + drift_ref[x, f] * (moved + flow)
-            carry[x] = carry[x] + cosine * flux
-            carry[SUB + x] = carry[SUB + x] + sine * flux
-            carry[2 * SUB + x] = carry[2 * SUB + x] + cosine * drift
-            carry[3 * SUB + x] = carry[3 * SUB + x] + sine * drift
-        return tuple(carry)
-
-    for x in range(SUB):
-        for f in range(groups):
-            drift_ref[x, f] = freq[3, f] * r_ref[x, f]
-    carry = lax.fori_loop(0, dirs, gather, (zero,) * (4 * SUB))
-
-    total = []
-    for j, value in enumerate(carry):
-        if j < 2 * SUB:
-            value = value * mask_b[j % SUB]
-        total.append(jnp.sum(value, axis=0, keepdims=True))
+                scale = mask_b[x] if c < 2 else r_ref[x, f]
+                value = value + acc[c, x, f] * (freq[3, f] * scale)
+            total.append(jnp.sum(value, axis=0, keepdims=True))
     total.append(jnp.zeros((128 - 4 * SUB, 128), jnp.float32))
     stacked = jnp.concatenate(total, axis=0)
     lat = lax.broadcasted_iota(jnp.int32, (128, 128), 0)
@@ -358,7 +364,7 @@
             pltpu.VMEM((2, 12, SUB, lats), f32),
             pltpu.VMEM((12, SUB, lats), f32),
             pltpu.VMEM((16, groups, SUB, lats), f32),
-            pltpu.VMEM((SUB, groups, SUB, lats), f32),
+            pltpu.VMEM((4, SUB, groups, SUB, lats), f32),
             pltpu.VMEM((2, SUB, lats), f32),
             pltpu.VMEM((2, 2, SUB, lats), f32),
             pltpu.VMEM((128, 128), f32),

time: 48.2 us -> 49.9 us (1.035)
  Pallas kernels: 42.4 us -> 44.1 us
    pallas_call x1, Pallas kernels: 42.4 us -> 44.1 us  [per_device(): pl.pallas_call(functools.partial(kernel, n, dirs, groups), out_shape=(jax...]
where the time goes in v4:
time: 49.9 us; the launch traced here: 49.6 us
  Pallas kernels  44.1 us (88%)
  local copies, waits for them, and re-layouts  4.82 us (10%)
  between operations  0.65 us (1%)
    pallas_call x1, Pallas kernels, per_device(): pl.pallas_call(functools.partial(kernel, n, dirs, groups), out_shape=(jax...  44.1 us
    unnamed x8, local copies, waits for them, and re-layouts  4.82 us

profile of v4, /device:TPU:0, one launch (start us, length us, event | category | flops | bytes accessed | tf_op | source)
XLA Modules:
  0.0 49.6 jit_solution(14075407892975202062)
XLA Ops:
  0.6 0.0 copy-start
  0.6 0.7 %copy-done = f32[2,8,128]{2,1,0:T(8,128)S(1)} copy-done((f32[2,8,128]{2,1,0:T(8,128)S(1)}, f32[2,8,128]{2,1,0:T(8,128)}, u32[]{:S(2)}) %copy-start) | copy-done | bytes 8216
  1.3 0.0 copy-start.1
  1.3 0.7 %copy-done.1 = s32[8,128]{1,0:T(8,128)S(1)} copy-done((s32[8,128]{1,0:T(8,128)S(1)}, s32[8,128]{1,0:T(8,128)}, u32[]{:S(2)}) %copy-start.1) | copy-done | bytes 4120
  2.0 0.0 copy-start.2
  2.0 0.7 %copy-done.2 = s32[128]{0:T(128)S(1)} copy-done((s32[128]{0:T(128)S(1)}, s32[128]{0:T(128)}, u32[]{:S(2)}) %copy-start.2) | copy-done | bytes 536
  2.7 44.1 %wave_window.1 = (f32[9216,128]{1,0:T(8,128)S(1)}, f32[4,8,128]{2,1,0:T(8,128)S(1)}) custom-call(f32[9216,128]{1,0:T(8,128)} %bitcast.5, f32[2,8,128]{2,1,0:T(8,128)S(1)} %copy-done, s32[8,128]{1,0:T(8,128)S(1)} %copy-done.1, s32[1,128]{1,0:T(1,128)S(1)} %bitcast.4), custom_call_target="tpu_custom_call" | custom-call | tf_op jit(solution)/shard_map/wave_window/pallas_call | solution.py:343
  46.8 2.2 %copy.8 = f32[36,32,8,128]{3,2,1,0:T(8,128)} copy(f32[36,32,8,128]{3,2,1,0:T(8,128)S(1)} %bitcast.3) | data formatting | bytes 9437184
  49.0 0.6 %copy.9 = f32[4,8,128]{2,1,0:T(8,128)} copy(f32[4,8,128]{2,1,0:T(8,128)S(1)} %get-tuple-element.9) | data formatting | bytes 32768
Async XLA Ops:
  0.6 0.7 %copy-start = (f32[2,8,128]{2,1,0:T(8,128)S(1)}, f32[2,8,128]{2,1,0:T(8,128)}, u32[]{:S(2)}) copy-start(f32[2,8,128]{2,1,0:T(8,128)} %wind_in.1) | copy-start | bytes 24580
  1.3 0.7 %copy-start.1 = (s32[8,128]{1,0:T(8,128)S(1)}, s32[8,128]{1,0:T(8,128)}, u32[]{:S(2)}) copy-start(s32[8,128]{1,0:T(8,128)} %land_in.1) | copy-start | bytes 12292
  2.0 0.7 %copy-start.2 = (s32[128]{0:T(128)S(1)}, s32[128]{0:T(128)}, u32[]{:S(2)}) copy-start(s32[128]{0:T(128)} %param.7) | copy-start | bytes 1540

commit v5 on v3

--- a/solution.py
+++ b/solution.py
@@ -152,7 +152,7 @@
                         sums[x] = sums[x] + new
                 return tuple(sums)
 
-            sums = lax.fori_loop(0, 2 * quarter, body, tuple(sums))
+            sums = lax.fori_loop(0, 2 * quarter, body, tuple(sums), unroll=2)
         return sums
 
     def fix(step, sums):
@@ -190,9 +190,9 @@
                 return total
 
             if east:
-                first = lax.fori_loop(0, 2 * quarter, body, first)
+                first = lax.fori_loop(0, 2 * quarter, body, first, unroll=3)
             else:
-                last = lax.fori_loop(0, 2 * quarter, body, last)
+                last = lax.fori_loop(0, 2 * quarter, body, last, unroll=3)
         return (first,) + tuple(sums[1:-1]) + (last,)
 
     def energy_tile(sums):
@@ -267,7 +267,7 @@
     for x in range(SUB):
         for f in range(groups):
             drift_ref[x, f] = freq[3, f] * r_ref[x, f]
-    carry = lax.fori_loop(0, dirs, gather, (zero,) * (4 * SUB))
+    carry = lax.fori_loop(0, dirs, gather, (zero,) * (4 * SUB), unroll=2)
 
     total = []
     for j, value in enumerate(carry):
@@ -312,7 +312,7 @@
                     moved * (1.0 + g_ref[at]) * r_ref[x, f])
         return 0
 
-    lax.fori_loop(0, dirs, write, 0)
+    lax.fori_loop(0, dirs, write, 0, unroll=2)
     lax.fori_loop(1, n, finish, 0)
     per_tile = 128 // SUB
     block = lax.broadcasted_iota(jnp.int32, (band, 128), 1) // SUB

time: 48.2 us -> 42.6 us (0.88)
  Pallas kernels: 42.4 us -> 36.8 us
    pallas_call x1, Pallas kernels: 42.4 us -> 36.8 us  [per_device(): pl.pallas_call(functools.partial(kernel, n, dirs, groups), out_shape=(jax...]
where the time goes in v5:
time: 42.6 us; the launch traced here: 42.3 us
  Pallas kernels  36.8 us (86%)
  local copies, waits for them, and re-layouts  4.82 us (11%)
  between operations  0.65 us (2%)
    pallas_call x1, Pallas kernels, per_device(): pl.pallas_call(functools.partial(kernel, n, dirs, groups), out_shape=(jax...  36.8 us
    unnamed x8, local copies, waits for them, and re-layouts  4.82 us

profile of v5, /device:TPU:0, one launch (start us, length us, event | category | flops | bytes accessed | tf_op | source)
XLA Modules:
  0.0 42.3 jit_solution(2393376015990438782)
XLA Ops:
  0.6 0.0 copy-start
  0.6 0.7 %copy-done = f32[2,8,128]{2,1,0:T(8,128)S(1)} copy-done((f32[2,8,128]{2,1,0:T(8,128)S(1)}, f32[2,8,128]{2,1,0:T(8,128)}, u32[]{:S(2)}) %copy-start) | copy-done | bytes 8216
  1.3 0.0 copy-start.1
  1.3 0.7 %copy-done.1 = s32[8,128]{1,0:T(8,128)S(1)} copy-done((s32[8,128]{1,0:T(8,128)S(1)}, s32[8,128]{1,0:T(8,128)}, u32[]{:S(2)}) %copy-start.1) | copy-done | bytes 4120
  2.0 0.0 copy-start.2
  2.0 0.7 %copy-done.2 = s32[128]{0:T(128)S(1)} copy-done((s32[128]{0:T(128)S(1)}, s32[128]{0:T(128)}, u32[]{:S(2)}) %copy-start.2) | copy-done | bytes 536
  2.7 36.8 %wave_window.1 = (f32[9216,128]{1,0:T(8,128)S(1)}, f32[4,8,128]{2,1,0:T(8,128)S(1)}) custom-call(f32[9216,128]{1,0:T(8,128)} %bitcast.5, f32[2,8,128]{2,1,0:T(8,128)S(1)} %copy-done, s32[8,128]{1,0:T(8,128)S(1)} %copy-done.1, s32[1,128]{1,0:T(1,128)S(1)} %bitcast.4), custom_call_target="tpu_custom_call" | custom-call | tf_op jit(solution)/shard_map/wave_window/pallas_call | solution.py:337
  39.5 2.2 %copy.8 = f32[36,32,8,128]{3,2,1,0:T(8,128)} copy(f32[36,32,8,128]{3,2,1,0:T(8,128)S(1)} %bitcast.3) | data formatting | bytes 9437184
  41.7 0.6 %copy.9 = f32[4,8,128]{2,1,0:T(8,128)} copy(f32[4,8,128]{2,1,0:T(8,128)S(1)} %get-tuple-element.9) | data formatting | bytes 32768
Async XLA Ops:
  0.6 0.7 %copy-start = (f32[2,8,128]{2,1,0:T(8,128)S(1)}, f32[2,8,128]{2,1,0:T(8,128)}, u32[]{:S(2)}) copy-start(f32[2,8,128]{2,1,0:T(8,128)} %wind_in.1) | copy-start | bytes 24580
  1.3 0.7 %copy-start.1 = (s32[8,128]{1,0:T(8,128)S(1)}, s32[8,128]{1,0:T(8,128)}, u32[]{:S(2)}) copy-start(s32[8,128]{1,0:T(8,128)} %land_in.1) | copy-start | bytes 12292
  2.0 0.7 %copy-start.2 = (s32[128]{0:T(128)S(1)}, s32[128]{0:T(128)}, u32[]{:S(2)}) copy-start(s32[128]{0:T(128)} %param.7) | copy-start | bytes 1540
